TPU v7x, 32 devices: a whole 2x2x4 slice. The times are simulated.
32 devices in a mesh: data: 4 (over z), model: 8 (over y, x, core).
Axes of the slice: x: 2, y: 2, z: 4, core: 2. Of those that a mesh axis runs over, the one named last changes fastest.
Arguments:
- hidden: bfloat16 [8192, 3072], P('data', 'model')
- unembed: bfloat16 [128256, 3072], P('model', 'data')
- draft_ids: int32 [8192], P('data')
- q_prob: float32 [8192], P('data')
Outputs:
- output 1: float32 [8192], P('data')
- output 2: float32 [8192], P('data')
All inputs are finite; a program needn't handle non-finite values.
Results may differ from a plain program's by a relative error of at most 0.001.
Values are sent between devices in bfloat16 or wider.
A program may use at most 1 GiB of HBM per device.

v0:
```python
import jax
import jax.numpy as jnp
from jax import lax
from jax.sharding import PartitionSpec as P


def solution(mesh):
    def per_device(h_part, w_part, draft_loc, q_loc):
        h_rows = lax.all_gather(h_part, "model", axis=1, tiled=True)
        w_rows = lax.all_gather(w_part, "data", axis=1, tiled=True)
        logits = lax.dot_general(h_rows, w_rows, (((1,), (1,)), ((), ())), preferred_element_type=jnp.float32)
        shard_vocab = w_rows.shape[0]
        row_max = lax.pmax(jnp.max(logits, axis=1), "model")
        local_sum = jnp.sum(jnp.exp(logits - row_max[:, None]), axis=1)
        vocab_ids = lax.axis_index("model") * shard_vocab + lax.broadcasted_iota(jnp.int32, (1, shard_vocab), 1)
        local_pick = jnp.sum(jnp.where(vocab_ids == draft_loc[:, None], logits, 0.0), axis=1)
        totals = lax.psum(jnp.stack([local_sum, local_pick]), "model")
        log_prob = totals[1] - row_max - jnp.log(totals[0])
        accept = jnp.minimum(1.0, jnp.exp(log_prob) / q_loc)
        return log_prob, accept

    return jax.shard_map(per_device, mesh=mesh, in_specs=(P("data", "model"), P("model", "data"), P("data"), P("data")), out_specs=(P("data"), P("data")), check_vma=False)
```

profile of v0, /device:TPU:0, one launch (start us, length us, event | category | flops | bytes accessed | tf_op | source)
XLA Modules:
  0.0 2017.8 jit_solution(15685521493353820095)
XLA Ops:
  7.2 0.0 all-gather.3.cloned.1.call-start
  7.2 0.7 all-gather.3.cloned.1.call-update
  7.9 0.0 all-gather.5.cloned.1.call-start
  7.9 0.7 all-gather.5.cloned.1.call-update
  8.7 0.6 iota_add_fusion
  9.3 77.6 %all-gather.3.cloned.1.call-done = bf16[2048,3072]{1,0:T(8,128)(2,1)} async-done(((bf16[2048,384]{1,0:T(8,128)(2,1)}), bf16[2048,3072]{1,0:T(8,128)(2,1)}) %all-gather.3.cloned.1.call-update) | async-done | bytes 12582928 | tf_op jit(solution)/shard_map/all_gather | solution.py:9
  86.9 1627.4 %all-gather.5.cloned.1.call-done = bf16[16032,3072]{1,0:T(8,128)(2,1)} async-done(((bf16[16032,768]{1,0:T(8,128)(2,1)}), bf16[16032,3072]{1,0:T(8,128)(2,1)}) %all-gather.5.cloned.1.call-update) | async-done | bytes 98500624 | tf_op jit(solution)/shard_map/all_gather | solution.py:10
  1714.4 0.0 copy-start
  1714.4 0.0 copy-start.1
  1714.4 218.6 %fusion.1 = (f32[2048]{0:T(1024)S(1)}, f32[2048,16032]{0,1:T(8,128)}) fusion(bf16[2048,3072]{1,0:T(8,128)(2,1)} %all-gather.3.cloned.1.call-done, bf16[16032,3072]{1,0:T(8,128)(2,1)} %all-gather.5.cloned.1.call-done), kind=kOutput, calls=%fused_computation.8 | convolution fusion | flops 201762078720 | bytes 242425856 | tf_op jit(solution)/shard_map/dot_general | solution.py:11
  1932.9 0.0 copy-start.2
  1932.9 14.1 pmax.7
  1947.1 0.0 copy-done
  1947.1 0.0 copy-done.1
  1947.1 40.8 %exponential_reduce_fusion = (f32[2048]{0:T(1024)S(1)}, f32[2048]{0:T(1024)S(1)}) fusion(f32[2048,16032]{0,1:T(8,128)} %get-tuple-element.9, f32[2048]{0:T(1024)S(1)} %pmax.7, s32[2048]{0:T(1024)S(1)} %copy-done.1, s32[16032]{0:T(1024)S(1)} %copy-done), kind=kLoop, calls=%fused_computation.1 | loop fusion | flops 164163584 | bytes 131431040 | tf_op jit(solution)/shard_map/reduce_sum | solution.py:14
  1988.0 22.3 %psum.7 = f32[2,2048]{1,0:T(2,128)S(1)} all-reduce(f32[2,2048]{1,0:T(2,128)S(1)} %pad_maximum_fusion), channel_id=1, replica_groups=mesh['data'=4,'model'=8] {'model'}, use_global_device_ids=true, to_apply=%region_4.5 | all-reduce | flops 4096 | bytes 32768 | tf_op jit(solution)/shard_map/psum | solution.py:17
  2010.3 0.0 copy-done.2
  2010.3 0.6 divide_minimum_fusion
  (2 shorter events, 0.0 us)
Async XLA Ops:
  7.2 79.8 %all-gather.3.cloned.1.call-start = ((), (), s32[]{:S(2)}) async-start(), calls=%async_computation | async-start | bytes 14155776 | tf_op jit(solution)/shard_map/all_gather | solution.py:9
  7.9 1706.5 %all-gather.5.cloned.1.call-start = ((), (), s32[]{:S(2)}) async-start(), calls=%async_computation.1 | async-start | bytes 123125760 | tf_op jit(solution)/shard_map/all_gather | solution.py:10
  1714.4 232.7 %copy-start = (s32[16032]{0:T(1024)S(1)}, s32[16032]{0:T(1024)}, u32[]{:S(2)}) copy-start(s32[16032]{0:T(1024)} %iota_add_fusion) | copy-start | bytes 192388
  1714.4 232.7 %copy-start.1 = (s32[2048]{0:T(1024)S(1)}, s32[2048]{0:T(1024)}, u32[]{:S(2)}) copy-start(s32[2048]{0:T(1024)} %param.6) | copy-start | bytes 24580
  1932.9 77.4 %copy-start.2 = (f32[2048]{0:T(1024)S(1)}, f32[2048]{0:T(1024)}, u32[]{:S(2)}) copy-start(f32[2048]{0:T(1024)} %param.7) | copy-start | bytes 24580
Sparse Core Ops, SparseCore 0:
  9.8 77.0 all-gather.2
  88.5 1625.8 all-gather.4
where the time goes:
time: 2020 us
  waiting for transfers between devices  1710 us (85%)
  matrix products  219 us (11%)
  other arithmetic  42.1 us (2%)
  blocking collectives  36.4 us (2%)
    all_gather x1, waiting for transfers between devices, per_device(): w_rows = lax.all_gather(w_part, 'data', axis=1, tiled=True)  1630 us
    dot_general x1, matrix products, per_device(): lax.dot_general(h_rows, w_rows, (((1,), (1,)), ((), ())), preferred_eleme...  219 us
    all_gather x1, waiting for transfers between devices, per_device(): h_rows = lax.all_gather(h_part, 'model', axis=1, tiled=True)  77.6 us
    reduce_sum x1, other arithmetic, per_device(): local_sum = jnp.sum(jnp.exp(logits - row_max[:, None]), axis=1)  40.8 us
  transfers between devices with their start and end apart: 2, of which 2 were waited for; matrix products, arithmetic and copies ran while one was open for 0% of the time, Pallas kernels for 0%

commit v1 on v0

v1 whole, which is shorter than its diff:
```python
import functools

import jax
import jax.numpy as jnp
from jax import lax
from jax.experimental import pallas as pl
from jax.experimental.pallas import tpu as pltpu
from jax.sharding import PartitionSpec as P

MESH = pl.DeviceIdType.MESH
NZ = 4
NM = 8
OFFSETS = (-1, 1, -2, 2, -3, 3)
BLOCK = 256


def chunk_plan(piece, big, tails):
    count = (piece - sum(tails)) // big
    assert count * big + sum(tails) == piece
    starts, at = [], count * big
    for size in tails:
        starts.append((at, size))
        at += size
    return count, starts


def kernel(
    cfg, h_ref, w_ref, draft_ref, stats_ref, land_ref,
    hv, wb, dv, m_acc, s_acc, p_acc,
    loc_sem, dr_s, dr_r, hz_s, hz_r, hx_s, hx_r, hy_s, hy_r, dx_s, dx_r, dy_s, dy_r, hp_s, hp_r, w_s, w_r, ld_sem,
):
    slab, part, piece, step, shard, width, big, count, tails = cfg
    d = lax.axis_index("data")
    m = lax.axis_index("model")
    xn = m + 2 - 4 * ((m // 2) % 2)
    yn = m + 4 - 8 * (m // 4)
    xy = xn + 4 - 8 * (xn // 4)
    pn = m + 1 - 2 * (m % 2)

    barrier = pltpu.get_barrier_semaphore()
    for j in (1, 2, 3):
        pl.semaphore_signal(barrier, inc=1, device_id=(lax.rem(d + j, NZ), m), device_id_type=MESH)
    for other in (xn, yn, pn):
        pl.semaphore_signal(barrier, inc=1, device_id=(d, other), device_id_type=MESH)
    pl.semaphore_wait(barrier, 6)

    def spot(s, mm):
        return hv.at[pl.ds(pl.multiple_of(s * slab, slab), slab), pl.ds(pl.multiple_of(mm * part, part), part)]

    def half(s, mm, which):
        rows = slab // 2
        return hv.at[pl.ds(pl.multiple_of(s * slab + which * rows, rows), rows), pl.ds(pl.multiple_of(mm * part, part), part)]

    def remote(src, dst, ssem, rsem, to):
        return pltpu.make_async_remote_copy(src_ref=src, dst_ref=dst, send_sem=ssem, recv_sem=rsem, device_id=to, device_id_type=MESH)

    def piece_start(t):
        return step * t + (piece - step) * (t // 3)

    def w_copy(j, idx, c0, size):
        t = lax.rem(d + j, NZ)
        return remote(
            w_ref.at[pl.ds(pl.multiple_of(piece_start(t) + c0, 16), size), :],
            land_ref.at[pl.ds(pl.multiple_of(c0, 16), size), pl.ds(pl.multiple_of(d * width, width), width)],
            w_s.at[j - 1, idx], w_r.at[j - 1, idx], (t, m),
        )

    def hz_copy(src, s, ssem, to):
        return remote(src, spot(s, m), ssem, hz_r.at[s], (to, m))

    def hx_copy(src, s):
        return remote(src, spot(s, m), hx_s.at[s], hx_r.at[s], (d, xn))

    def hy_copy(src, s):
        return remote(src, spot(s, m), hy_s.at[s], hy_r.at[s], (d, yn))

    def dx_copy(s):
        return remote(half(s, yn, 0), half(s, yn, 0), dx_s.at[s], dx_r.at[s], (d, xn))

    def dy_copy(s):
        return remote(half(s, xn, 1), half(s, xn, 1), dy_s.at[s], dy_r.at[s], (d, yn))

    def hp_copy(src, s, mm, k):
        return remote(src, spot(s, mm), hp_s.at[s, k], hp_r.at[s, k], (d, pn))

    own = pltpu.make_async_copy(h_ref, spot(d, m), loc_sem.at[0])
    own.start()
    own_draft = pltpu.make_async_copy(draft_ref, dv.at[d], loc_sem.at[1])
    own_draft.start()

    @pl.when(d < NZ - 1)
    def _():
        hz_copy(h_ref, d, hz_s.at[d], d + 1).start()

    @pl.when(d > 0)
    def _():
        hz_copy(h_ref, d, hz_s.at[NZ], d - 1).start()

    hx_copy(h_ref, d).start()
    hy_copy(h_ref, d).start()
    hp_copy(h_ref, d, m, 0).start()
    drafts = [
        remote(draft_ref, dv.at[d], dr_s.at[j - 1], dr_r.at[j - 1], (lax.rem(d + j, NZ), m)) for j in (1, 2, 3)
    ]
    for copy in drafts:
        copy.start()

    spans = [(c * big, big) for c in range(count)] + list(tails)

    def send_weights(lo, hi):
        for idx in range(lo, hi):
            for j in (2, 1, 3):
                w_copy(j, idx, *spans[idx]).start()

    for o in OFFSETS:
        s = d + o

        @pl.when((s >= 0) & (s < NZ))
        def _(o=o, s=s):
            src = spot(s, m)
            hz_copy(src, s, hz_s.at[s], d + (1 if o < 0 else -1)).wait_recv()
            if o < 0:
                @pl.when(d < NZ - 1)
                def _():
                    hz_copy(src, s, hz_s.at[s], d + 1).start()
            else:
                @pl.when(d > 0)
                def _():
                    hz_copy(src, s, hz_s.at[s], d - 1).start()
            hx_copy(src, s).start()
            hy_copy(src, s).start()
            hp_copy(src, s, m, 0).start()

        if o == 1:
            send_weights(0, 1)
        if o == 2:
            send_weights(1, len(spans))

    for o in (0,) + OFFSETS:
        s = d + o

        @pl.when((s >= 0) & (s < NZ))
        def _(s=s):
            hx_copy(spot(s, m), s).wait_recv()
            dy_copy(s).start()
            hp_copy(spot(s, xn), s, xn, 1).start()
            hy_copy(spot(s, m), s).wait_recv()
            dx_copy(s).start()
            hp_copy(spot(s, yn), s, yn, 2).start()

    for o in (0,) + OFFSETS:
        s = d + o

        @pl.when((s >= 0) & (s < NZ))
        def _(s=s):
            dx_copy(s).wait_recv()
            dy_copy(s).wait_recv()
            hp_copy(spot(s, xy), s, xy, 3).start()

    m_acc[...] = jnp.full(m_acc.shape, -jnp.inf, jnp.float32)
    s_acc[...] = jnp.zeros_like(s_acc)
    p_acc[...] = jnp.zeros_like(p_acc)

    own.wait()
    own_draft.wait()
    for copy in drafts:
        copy.wait()
    for s in range(NZ):
        for k in range(4):
            hp_copy(spot(s, m), s, m, k).wait_recv()

    base = m * shard + piece_start(d)
    limit = step + (piece - step) * (d // 2)

    def work(idx, c0, size, last):
        loads = [
            pltpu.make_async_copy(
                w_ref.at[pl.ds(pl.multiple_of(piece_start(d) + c0, 16), size), :],
                wb.at[pl.ds(0, size), pl.ds(pl.multiple_of(d * width, width), width)],
                ld_sem.at[0],
            )
        ]
        loads[0].start()
        for j in (1, 2, 3):
            w_copy(j, idx, c0, size).wait_recv()
            cols = pl.ds(pl.multiple_of(lax.rem(d + NZ - j, NZ) * width, width), width)
            copy = pltpu.make_async_copy(
                land_ref.at[pl.ds(pl.multiple_of(c0, 16), size), cols], wb.at[pl.ds(0, size), cols], ld_sem.at[j]
            )
            copy.start()
            loads.append(copy)
        for copy in loads:
            copy.wait()

        per = slab // BLOCK

        def block(n, carry):
            rows = pl.multiple_of(n * BLOCK, BLOCK)
            logits = lax.dot_general(
                wb[pl.ds(0, size), :], hv[pl.ds(rows, BLOCK), :], (((1,), (1,)), ((), ())),
                preferred_element_type=jnp.float32,
            )
            tiles = logits.reshape(size // 8, 8, BLOCK)
            ids = 8 * lax.broadcasted_iota(jnp.int32, tiles.shape, 0) + lax.broadcasted_iota(jnp.int32, tiles.shape, 1)
            want = dv[n // per, :, pl.ds(pl.multiple_of((n % per) * BLOCK, BLOCK), BLOCK)] - (base + c0)
            if last:
                tiles = jnp.where(ids < limit - c0, tiles, -jnp.inf)
                want = jnp.where(want < limit - c0, want, -1)
            cols = pl.ds(rows, BLOCK)
            old = m_acc[:, cols]
            new = jnp.maximum(old, jnp.max(tiles, axis=0))
            m_acc[:, cols] = new
            s_acc[:, cols] = s_acc[:, cols] * jnp.exp(old - new) + jnp.sum(jnp.exp(tiles - new[None]), axis=0)
            p_acc[:, cols] = p_acc[:, cols] + jnp.sum(jnp.where(ids == want[None], tiles, 0.0), axis=0)
            return carry

        lax.fori_loop(0, NZ * per, block, 0)

    def big_chunk(c, carry):
        work(c, c * big, big, False)
        return carry

    lax.fori_loop(0, count, big_chunk, 0)
    for k, (c0, size) in enumerate(tails):
        work(count + k, c0, size, k == len(tails) - 1)

    top = jnp.max(m_acc[...], axis=0, keepdims=True)
    stats_ref[0:1, :] = top
    stats_ref[1:2, :] = jnp.sum(s_acc[...] * jnp.exp(m_acc[...] - top), axis=0, keepdims=True)
    stats_ref[2:3, :] = jnp.sum(p_acc[...], axis=0, keepdims=True)

    for idx, span in enumerate(spans):
        for j in (1, 2, 3):
            w_copy(j, idx, *span).wait_send()

    @pl.when(d < NZ - 1)
    def _():
        hz_copy(h_ref, d, hz_s.at[d], d + 1).wait_send()

    @pl.when(d > 0)
    def _():
        hz_copy(h_ref, d, hz_s.at[NZ], d - 1).wait_send()

    for o in OFFSETS:
        s = d + o
        on = (s >= 0) & (d < NZ - 1) if o < 0 else (s < NZ) & (d > 0)

        @pl.when(on)
        def _(o=o, s=s):
            hz_copy(spot(s, m), s, hz_s.at[s], d + (1 if o < 0 else -1)).wait_send()

    for s in range(NZ):
        hx_copy(spot(s, m), s).wait_send()
        hy_copy(spot(s, m), s).wait_send()
        dx_copy(s).wait_send()
        dy_copy(s).wait_send()
        for k in range(4):
            hp_copy(spot(s, m), s, m, k).wait_send()


def solution(mesh):
    def per_device(h_part, w_part, draft_loc, q_loc):
        slab, part = h_part.shape
        shard, width = w_part.shape
        rows, full = slab * NZ, part * NM
        step = shard // NZ // 16 * 16
        piece = shard - 3 * step - ((shard - 3 * step) - step) // 2
        big = 512
        tails = (256, piece - 256 - (piece - 256 - 160) // big * big)
        count, tail_spans = chunk_plan(piece, big, tails)
        n_chunks = count + len(tails)
        cfg = (slab, part, piece, step, shard, width, big, count, tuple(tail_spans))
        dma = pltpu.SemaphoreType.DMA
        stats, _ = pl.pallas_call(
            functools.partial(kernel, cfg),
            out_shape=(
                jax.ShapeDtypeStruct((3, rows), jnp.float32),
                jax.ShapeDtypeStruct((piece, full), jnp.bfloat16),
            ),
            in_specs=[pl.BlockSpec(memory_space=pl.ANY)] * 3,
            out_specs=(pl.BlockSpec(memory_space=pltpu.VMEM), pl.BlockSpec(memory_space=pl.ANY)),
            scratch_shapes=[
                pltpu.VMEM((rows, full), jnp.bfloat16),
                pltpu.VMEM((big, full), jnp.bfloat16),
                pltpu.VMEM((NZ, 1, slab), jnp.int32),
                pltpu.VMEM((8, rows), jnp.float32),
                pltpu.VMEM((8, rows), jnp.float32),
                pltpu.VMEM((8, rows), jnp.float32),
                dma((2,)), dma((3,)), dma((3,)), dma((NZ + 1,)), dma((NZ,)),
                dma((NZ,)), dma((NZ,)), dma((NZ,)), dma((NZ,)),
                dma((NZ,)), dma((NZ,)), dma((NZ,)), dma((NZ,)),
                dma((NZ, 4)), dma((NZ, 4)), dma((3, n_chunks)), dma((3, n_chunks)), dma((4,)),
            ],
            compiler_params=pltpu.CompilerParams(
                collective_id=0, has_side_effects=True, vmem_limit_bytes=67043328
            ),
        )(h_part, w_part, draft_loc.reshape(1, slab))

        mine = lax.all_to_all(stats.reshape(3, NZ, slab).swapaxes(0, 1), "data", 0, 0)
        top = jnp.max(mine[:, 0], axis=0)
        total = jnp.sum(mine[:, 1] * jnp.exp(mine[:, 0] - top), axis=0)
        both = lax.all_gather(jnp.stack([top, total, jnp.sum(mine[:, 2], axis=0)]), "model", axis=0)
        row_max = jnp.max(both[:, 0], axis=0)
        row_sum = jnp.sum(both[:, 1] * jnp.exp(both[:, 0] - row_max), axis=0)
        log_prob = jnp.sum(both[:, 2], axis=0) - row_max - jnp.log(row_sum)
        accept = jnp.minimum(1.0, jnp.exp(log_prob) / q_loc)
        return log_prob, accept

    return jax.shard_map(per_device, mesh=mesh, in_specs=(P("data", "model"), P("model", "data"), P("data"), P("data")), out_specs=(P("data"), P("data")), check_vma=False)
```

time: 2020 us -> 699 us (0.35)
  waiting for transfers between devices: 1710 us -> 0 us
  Pallas kernels: 0 us -> 658 us
  matrix products: 219 us -> 0 us
  other arithmetic: 42.1 us -> 1.76 us
    all_gather x2 -> x0, waiting for transfers between devices: 1710 us -> none  [the longest x1 1630 us: per_device(): w_rows = lax.all_gather(w_part, 'data', axis=1, tiled=True)]
    pallas_call x0 -> x1, Pallas kernels: none -> 658 us  [per_device(): pl.pallas_call(functools.partial(kernel, cfg), out_shape=(jax.ShapeDtypeS...]
    dot_general x1 -> x0, matrix products: 219 us -> none  [per_device(): lax.dot_general(h_rows, w_rows, (((1,), (1,)), ((), ())), preferred_eleme...]
    reduce_sum x1 -> x3, other arithmetic: 40.8 us -> 0.3 us  [the longest x1 0.19 us: per_device(): log_prob = jnp.sum(both[:, 2], axis=0) - row_max - jnp.log(row_sum)]
    all_to_all x0 -> x1, blocking collectives: none -> 29.2 us  [per_device(): lax.all_to_all(stats.reshape(3, NZ, slab).swapaxes(0, 1), 'data', 0, 0)]
    psum x1 -> x0, blocking collectives: 22.3 us -> none  [per_device(): totals = lax.psum(jnp.stack([local_sum, local_pick]), 'model')]
  transfers between devices with their start and end apart: 2 -> 0, of which waited for: 2 -> 0; matrix products, arithmetic and copies ran while one was open for 0% -> 0% of each run, Pallas kernels for 0% -> 0%
where the time goes in v1:
time: 699 us; the launch traced here: 698 us
  Pallas kernels  658 us (94%)
  blocking collectives  38.5 us (6%)
    pallas_call x1, Pallas kernels, per_device(): pl.pallas_call(functools.partial(kernel, cfg), out_shape=(jax.ShapeDtypeS...  658 us
    all_to_all x1, blocking collectives, per_device(): lax.all_to_all(stats.reshape(3, NZ, slab).swapaxes(0, 1), 'data', 0, 0)  29.2 us

profile of v1, /device:TPU:0, one launch (start us, length us, event | category | flops | bytes accessed | tf_op | source)
XLA Modules:
  0.0 698.5 jit_solution(15074269064783100341)
XLA Ops:
  0.6 657.6 %shard_map.59 = (f32[3,8192]{1,0:T(4,128)}, bf16[4016,3072]{1,0:T(8,128)(2,1)}) custom-call(bf16[2048,384]{1,0:T(8,128)(2,1)} %h_ref.1, bf16[16032,768]{1,0:T(8,128)(2,1)} %w_ref.1, s32[1,2048]{1,0:T(1,128)} %bitcast.37), custom_call_target="tpu_custom_call" | custom-call | tf_op jit(solution)/shard_map/pallas_call | solution.py:274
  658.2 29.2 %all_to_all.5 = f32[4,3,2048]{2,1,0:T(4,128)S(1)} all-to-all(f32[4,3,2048]{2,1,0:T(4,128)} %bitcast.33), channel_id=1, replica_groups=mesh['data'=4,'model'=8] {'data'}, dimensions={0} | all-to-all | bytes 196608 | tf_op jit(solution)/shard_map/all_to_all | solution.py:299
  687.4 0.1 slice_reduce_fusion.2
  687.6 9.3 %all-gather.1 = f32[8,3,2048]{2,1,0:T(4,128)S(1)} all-gather(f32[1,3,2048]{2,1,0:T(4,128)S(1)} %maximum_bitcast_fusion), channel_id=2, replica_groups=mesh['data'=4,'model'=8] {'model'}, dimensions={0}, use_global_device_ids=true | all-gather | bytes 221184 | tf_op jit(solution)/shard_map/all_gather | solution.py:302
  696.9 0.2 slice_reduce_fusion
  697.1 0.1 fusion.1
  697.2 1.3 divide_minimum_fusion
  (2 shorter events, 0.1 us)

commit v2 on v1

v2 whole, which is shorter than its diff:
```python
import functools

import jax
import jax.numpy as jnp
from jax import lax
from jax.experimental import pallas as pl
from jax.experimental.pallas import tpu as pltpu
from jax.sharding import PartitionSpec as P

MESH = pl.DeviceIdType.MESH
NZ = 4
NM = 8
OFFSETS = (-1, 1, -2, 2, -3, 3)
BLOCK = 512
BIG = 288
AHEAD = 13


def merge(shares):
    shares = [jnp.split(s, 3, axis=1) for s in shares]
    top = functools.reduce(jnp.maximum, [s[0] for s in shares])
    return top, sum(s[1] * jnp.exp(s[0] - top) for s in shares), sum(s[2] for s in shares)


def kernel(
    cfg, h_ref, w_ref, draft_ref, q_ref, logp_ref, accept_ref, land_ref,
    hv, wb, dv, m_acc, s_acc, p_acc, even, odd, part_acc, stats, zin, gat,
    zx_s, zx_r, mx_s, mx_r, loc_sem, dr_s, dr_r, hz_s, hz_r, hx_s, hx_r, hy_s, hy_r, dx_s, dx_r, dy_s, dy_r, hp_s, hp_r, w_s, w_r, ld_sem,
):
    slab, part, piece, step, shard, width, big, count = cfg
    tail = piece - count * big
    d = lax.axis_index("data")
    m = lax.axis_index("model")
    xn = m + 2 - 4 * ((m // 2) % 2)
    yn = m + 4 - 8 * (m // 4)
    xy = xn + 4 - 8 * (xn // 4)
    pn = m + 1 - 2 * (m % 2)

    barrier = pltpu.get_barrier_semaphore()
    for j in (1, 2, 3):
        pl.semaphore_signal(barrier, inc=1, device_id=(lax.rem(d + j, NZ), m), device_id_type=MESH)
    for k in range(1, NM):
        pl.semaphore_signal(barrier, inc=1, device_id=(d, lax.rem(m + k, NM)), device_id_type=MESH)
    pl.semaphore_wait(barrier, NZ - 1 + NM - 1)

    def spot(s, mm):
        return hv.at[pl.ds(pl.multiple_of(s * slab, slab), slab), pl.ds(pl.multiple_of(mm * part, part), part)]

    def half(s, mm, which):
        rows = slab // 2
        return hv.at[pl.ds(pl.multiple_of(s * slab + which * rows, rows), rows), pl.ds(pl.multiple_of(mm * part, part), part)]

    def remote(src, dst, ssem, rsem, to):
        return pltpu.make_async_remote_copy(src_ref=src, dst_ref=dst, send_sem=ssem, recv_sem=rsem, device_id=to, device_id_type=MESH)

    def piece_start(t):
        return step * t + (piece - step) * (t // 3)

    def w_copy(j, idx, c0, size):
        t = lax.rem(d + j, NZ)
        return remote(
            w_ref.at[pl.ds(pl.multiple_of(piece_start(t) + c0, 16), size), :],
            land_ref.at[pl.ds(pl.multiple_of(c0, 16), size), pl.ds(pl.multiple_of(d * width, width), width)],
            w_s.at[j - 1, idx], w_r.at[j - 1, idx], (t, m),
        )

    def hz_copy(src, s, ssem, to):
        return remote(src, spot(s, m), ssem, hz_r.at[s], (to, m))

    def hx_copy(src, s):
        return remote(src, spot(s, m), hx_s.at[s], hx_r.at[s], (d, xn))

    def hy_copy(src, s):
        return remote(src, spot(s, m), hy_s.at[s], hy_r.at[s], (d, yn))

    def dx_copy(s):
        return remote(half(s, yn, 0), half(s, yn, 0), dx_s.at[s], dx_r.at[s], (d, xn))

    def dy_copy(s):
        return remote(half(s, xn, 1), half(s, xn, 1), dy_s.at[s], dy_r.at[s], (d, yn))

    def hp_copy(src, s, mm, k):
        return remote(src, spot(s, mm), hp_s.at[s, k], hp_r.at[s, k], (d, pn))

    own = pltpu.make_async_copy(h_ref, spot(d, m), loc_sem.at[0])
    own.start()
    own_draft = pltpu.make_async_copy(draft_ref, dv.at[d], loc_sem.at[1])
    own_draft.start()

    @pl.when(d < NZ - 1)
    def _():
        hz_copy(h_ref, d, hz_s.at[d], d + 1).start()

    @pl.when(d > 0)
    def _():
        hz_copy(h_ref, d, hz_s.at[NZ], d - 1).start()

    hx_copy(h_ref, d).start()
    hy_copy(h_ref, d).start()
    hp_copy(h_ref, d, m, 0).start()
    drafts = [
        remote(draft_ref, dv.at[d], dr_s.at[j - 1], dr_r.at[j - 1], (lax.rem(d + j, NZ), m)) for j in (1, 2, 3)
    ]
    for copy in drafts:
        copy.start()

    spans = [(c * big, big) for c in range(count)] + [(count * big, tail)]
    to_near, from_near = 1 + 2 * (d % 2), 3 - 2 * (d % 2)

    def send_weights(lo, hi):
        for idx in range(lo, hi):
            for j in (2, 1, 3):
                w_copy(j, idx, *spans[idx]).start()

    for o in OFFSETS:
        s = d + o

        @pl.when((s >= 0) & (s < NZ))
        def _(o=o, s=s):
            src = spot(s, m)
            hz_copy(src, s, hz_s.at[s], d + (1 if o < 0 else -1)).wait_recv()
            if o < 0:
                @pl.when(d < NZ - 1)
                def _():
                    hz_copy(src, s, hz_s.at[s], d + 1).start()
            else:
                @pl.when(d > 0)
                def _():
                    hz_copy(src, s, hz_s.at[s], d - 1).start()
            hx_copy(src, s).start()
            hy_copy(src, s).start()
            hp_copy(src, s, m, 0).start()

        if o == 1:
            send_weights(0, 1)
            w_copy(to_near, count, *spans[count]).start()
        if o == 2:
            send_weights(1, AHEAD)

    for o in (0,) + OFFSETS:
        s = d + o

        @pl.when((s >= 0) & (s < NZ))
        def _(s=s):
            hx_copy(spot(s, m), s).wait_recv()
            dy_copy(s).start()
            hp_copy(spot(s, xn), s, xn, 1).start()
            hy_copy(spot(s, m), s).wait_recv()
            dx_copy(s).start()
            hp_copy(spot(s, yn), s, yn, 2).start()

    for o in (0,) + OFFSETS:
        s = d + o

        @pl.when((s >= 0) & (s < NZ))
        def _(s=s):
            dx_copy(s).wait_recv()
            dy_copy(s).wait_recv()
            hp_copy(spot(s, xy), s, xy, 3).start()

    m_acc[...] = jnp.full(m_acc.shape, -jnp.inf, jnp.float32)
    s_acc[...] = jnp.zeros_like(s_acc)
    p_acc[...] = jnp.zeros_like(p_acc)

    own.wait()
    own_draft.wait()
    for copy in drafts:
        copy.wait()
    for s in range(NZ):
        for k in range(4):
            hp_copy(spot(s, m), s, m, k).wait_recv()

    base = m * shard + piece_start(d)
    limit = step + (piece - step) * (d // 2)

    per = slab // BLOCK
    blocks = NZ * per
    hw = 2 * width
    near = pl.ds(pl.multiple_of(d // 2 * hw, hw), hw)
    far = pl.ds(pl.multiple_of((1 - d // 2) * hw, hw), hw)

    def load(src, c0, size, cols, k):
        return pltpu.make_async_copy(src.at[pl.ds(pl.multiple_of(c0, 16), size), cols], wb.at[pl.ds(0, size), cols], ld_sem.at[k])

    def load_own(c0, size):
        cols = pl.ds(pl.multiple_of(d * width, width), width)
        return pltpu.make_async_copy(
            w_ref.at[pl.ds(pl.multiple_of(piece_start(d) + c0, 16), size), :], wb.at[pl.ds(0, size), cols], ld_sem.at[0]
        )

    def column(j):
        return pl.ds(pl.multiple_of(lax.rem(d + NZ - j, NZ) * width, width), width)

    def block_of(n):
        return pl.ds(pl.multiple_of(n * BLOCK, BLOCK), BLOCK)

    def product(n, size, cols):
        return lax.dot_general(
            wb[pl.ds(0, size), cols], hv[block_of(n), cols], (((1,), (1,)), ((), ())), preferred_element_type=jnp.float32
        )

    def fold(n, c0, size, ref, last):
        cols = block_of(n)
        tiles = ref[pl.ds(0, size), :].reshape(size // 8, 8, BLOCK)
        ids = 8 * lax.broadcasted_iota(jnp.int32, tiles.shape, 0) + lax.broadcasted_iota(jnp.int32, tiles.shape, 1)
        want = dv[n // per, :, pl.ds(pl.multiple_of((n % per) * BLOCK, BLOCK), BLOCK)] - (base + c0)
        if last:
            tiles = jnp.where(ids < limit - c0, tiles, -jnp.inf)
            want = jnp.where(want < limit - c0, want, -1)
        old = m_acc[:, cols]
        new = jnp.maximum(old, jnp.max(tiles, axis=0))
        m_acc[:, cols] = new
        s_acc[:, cols] = s_acc[:, cols] * jnp.exp(old - new) + jnp.sum(jnp.exp(tiles - new[None]), axis=0)
        p_acc[:, cols] = p_acc[:, cols] + jnp.sum(jnp.where(ids == want[None], tiles, 0.0), axis=0)

    def sweep(c0, size, fill, last):
        def pair(n, carry):
            fill(2 * n + 1, odd)
            fold(2 * n, c0, size, even, last)
            fill(2 * n + 2, even)
            fold(2 * n + 1, c0, size, odd, last)
            return carry

        fill(0, even)
        lax.fori_loop(0, blocks // 2 - 1, pair, 0)
        fill(blocks - 1, odd)
        fold(blocks - 2, c0, size, even, last)
        fold(blocks - 1, c0, size, odd, last)

    t0 = count * big
    loads = [load_own(t0, tail), load(land_ref, t0, tail, column(from_near), 1)]
    w_copy(from_near, count, t0, tail).wait_recv()
    for copy in loads:
        copy.start()
    for copy in loads:
        copy.wait()

    def first_half(n, carry):
        part_acc[:, block_of(n)] = product(n, tail, near)
        return carry

    lax.fori_loop(0, blocks, first_half, 0)

    def big_chunk(c, carry):
        c0 = c * big
        loads = [load_own(c0, big)]
        loads[0].start()
        for j in (1, 2, 3):
            w_copy(j, c, c0, big).wait_recv()
            loads.append(load(land_ref, c0, big, column(j), j))
            loads[-1].start()
        ahead = c + AHEAD

        @pl.when(ahead < count)
        def _():
            for j in (2, 1, 3):
                w_copy(j, ahead, ahead * big, big).start()

        @pl.when(ahead == count)
        def _():
            for j in (2, from_near):
                w_copy(j, count, t0, tail).start()

        for copy in loads:
            copy.wait()

        def fill(n, ref):
            ref[...] = product(n, big, slice(None))

        sweep(c0, big, fill, False)
        return carry

    lax.fori_loop(0, count, big_chunk, 0)

    for j in (2, to_near):
        w_copy(j, count, t0, tail).wait_recv()
    rest = load(land_ref, t0, tail, far, 1)
    rest.start()
    rest.wait()

    def fill_rest(n, ref):
        ref[pl.ds(0, tail), :] = part_acc[:, block_of(n)] + product(n, tail, far)

    sweep(t0, tail, fill_rest, True)

    def put(ref, at, *share):
        for k, value in enumerate(share):
            ref[at, :, pl.ds(k * slab, slab)] = value

    for t in range(NZ):
        cols = pl.ds(t * slab, slab)
        tops = m_acc[:, cols]
        top = jnp.max(tops, axis=0, keepdims=True)
        put(stats, t, top, jnp.sum(s_acc[:, cols] * jnp.exp(tops - top), axis=0, keepdims=True), jnp.sum(p_acc[:, cols], axis=0, keepdims=True))

    for idx, span in enumerate(spans):
        for j in (1, 2, 3):
            w_copy(j, idx, *span).wait_send()

    @pl.when(d < NZ - 1)
    def _():
        hz_copy(h_ref, d, hz_s.at[d], d + 1).wait_send()

    @pl.when(d > 0)
    def _():
        hz_copy(h_ref, d, hz_s.at[NZ], d - 1).wait_send()

    for o in OFFSETS:
        s = d + o
        on = (s >= 0) & (d < NZ - 1) if o < 0 else (s < NZ) & (d > 0)

        @pl.when(on)
        def _(o=o, s=s):
            hz_copy(spot(s, m), s, hz_s.at[s], d + (1 if o < 0 else -1)).wait_send()

    for s in range(NZ):
        hx_copy(spot(s, m), s).wait_send()
        hy_copy(spot(s, m), s).wait_send()
        dx_copy(s).wait_send()
        dy_copy(s).wait_send()
        for k in range(4):
            hp_copy(spot(s, m), s, m, k).wait_send()

    def zx_copy(j):
        t = lax.rem(d + j, NZ)
        return remote(stats.at[t], zin.at[j - 1], zx_s.at[j - 1], zx_r.at[j - 1], (t, m))

    def mx_copy(k):
        return remote(gat.at[m], gat.at[m], mx_s.at[k - 1], mx_r.at[k - 1], (d, lax.rem(m + k, NM)))

    for j in (2, 1, 3):
        zx_copy(j).start()
    for j in (1, 2, 3):
        zx_copy(j).wait()
    shares = [stats[d]] + [zin[j] for j in range(NZ - 1)]
    put(gat, m, *merge(shares))
    for k in range(1, NM):
        mx_copy(k).start()
    for k in range(1, NM):
        mx_copy(k).wait()
    top, total, picked = merge([gat[k] for k in range(NM)])
    log_prob = picked - top - jnp.log(total)
    logp_ref[...] = log_prob
    accept_ref[...] = jnp.minimum(1.0, jnp.exp(log_prob) / q_ref[...])


def solution(mesh):
    def per_device(h_part, w_part, draft_loc, q_loc):
        slab, part = h_part.shape
        shard, width = w_part.shape
        rows, full = slab * NZ, part * NM
        step = shard // NZ // 16 * 16
        piece = shard - 3 * step - ((shard - 3 * step) - step) // 2
        big, count = BIG, (piece - 1) // BIG
        n_chunks = count + 1
        cfg = (slab, part, piece, step, shard, width, big, count)
        dma = pltpu.SemaphoreType.DMA
        log_prob, accept, _ = pl.pallas_call(
            functools.partial(kernel, cfg),
            out_shape=(
                jax.ShapeDtypeStruct((1, slab), jnp.float32),
                jax.ShapeDtypeStruct((1, slab), jnp.float32),
                jax.ShapeDtypeStruct((piece, full), jnp.bfloat16),
            ),
            in_specs=[pl.BlockSpec(memory_space=pl.ANY)] * 3 + [pl.BlockSpec(memory_space=pltpu.VMEM)],
            out_specs=(
                pl.BlockSpec(memory_space=pltpu.VMEM),
                pl.BlockSpec(memory_space=pltpu.VMEM),
                pl.BlockSpec(memory_space=pl.ANY),
            ),
            scratch_shapes=[
                pltpu.VMEM((rows, full), jnp.bfloat16),
                pltpu.VMEM((big, full), jnp.bfloat16),
                pltpu.VMEM((NZ, 1, slab), jnp.int32),
                pltpu.VMEM((8, rows), jnp.float32),
                pltpu.VMEM((8, rows), jnp.float32),
                pltpu.VMEM((8, rows), jnp.float32),
                pltpu.VMEM((big, BLOCK), jnp.float32),
                pltpu.VMEM((big, BLOCK), jnp.float32),
                pltpu.VMEM((piece - count * big, rows), jnp.float32),
                pltpu.VMEM((NZ, 1, 3 * slab), jnp.float32),
                pltpu.VMEM((NZ - 1, 1, 3 * slab), jnp.float32),
                pltpu.VMEM((NM, 1, 3 * slab), jnp.float32),
                dma((NZ - 1,)), dma((NZ - 1,)), dma((NM - 1,)), dma((NM - 1,)),
                dma((2,)), dma((3,)), dma((3,)), dma((NZ + 1,)), dma((NZ,)),
                dma((NZ,)), dma((NZ,)), dma((NZ,)), dma((NZ,)),
                dma((NZ,)), dma((NZ,)), dma((NZ,)), dma((NZ,)),
                dma((NZ, 4)), dma((NZ, 4)), dma((3, n_chunks)), dma((3, n_chunks)), dma((4,)),
            ],
            compiler_params=pltpu.CompilerParams(
                collective_id=0, has_side_effects=True, vmem_limit_bytes=67043328
            ),
        )(h_part, w_part, draft_loc.reshape(1, slab), q_loc.reshape(1, slab))
        return log_prob.reshape(slab), accept.reshape(slab)

    return jax.shard_map(per_device, mesh=mesh, in_specs=(P("data", "model"), P("model", "data"), P("data"), P("data")), out_specs=(P("data"), P("data")), check_vma=False)
```

time: 699 us -> 630 us (0.901)
  blocking collectives: 38.5 us -> 0 us
  Pallas kernels: 658 us -> 626 us
    pallas_call x1, Pallas kernels: 658 us -> 626 us  [per_device(): pl.pallas_call(functools.partial(kernel, cfg), out_shape=(jax.ShapeDtypeS...]
    all_to_all x1 -> x0, blocking collectives: 29.2 us -> none  [per_device(): lax.all_to_all(stats.reshape(3, NZ, slab).swapaxes(0, 1), 'data', 0, 0)]
    all_gather x1 -> x0, blocking collectives: 9.3 us -> none  [per_device(): lax.all_gather(jnp.stack([top, total, jnp.sum(mine[:, 2], axis=0)]), 'mod...]
where the time goes in v2:
time: 630 us
  Pallas kernels  626 us (99%)
    pallas_call x1, Pallas kernels, per_device(): pl.pallas_call(functools.partial(kernel, cfg), out_shape=(jax.ShapeDtypeS...  626 us

profile of v2, /device:TPU:0, one launch (start us, length us, event | category | flops | bytes accessed | tf_op | source)
XLA Modules:
  0.0 629.6 jit_solution(5251743876658990472)
XLA Ops:
  0.6 626.4 %shard_map.59 = (f32[1,2048]{1,0:T(1,128)}, f32[1,2048]{1,0:T(1,128)}, bf16[4016,3072]{1,0:T(8,128)(2,1)}) custom-call(bf16[2048,384]{1,0:T(8,128)(2,1)} %h_ref.1, bf16[16032,768]{1,0:T(8,128)(2,1)} %w_ref.1, s32[1,2048]{1,0:T(1,128)} %bitcast.4, f32[1,2048]{1,0:T(1,128)} %bitcast.5), custom_call_target="tpu_custom_call" | custom-call | tf_op jit(solution)/shard_map/pallas_call | solution.py:358
  627.0 1.3 copy.8
  628.3 1.3 copy.9

commit v3 on v2

--- a/solution.py
+++ b/solution.py
@@ -13,13 +13,13 @@
 OFFSETS = (-1, 1, -2, 2, -3, 3)
 BLOCK = 512
 BIG = 288
-AHEAD = 13
+LATE = 2
 
 
 def merge(shares):
-    shares = [jnp.split(s, 3, axis=1) for s in shares]
+    shares = [jnp.split(s, 2, axis=1) for s in shares]
     top = functools.reduce(jnp.maximum, [s[0] for s in shares])
-    return top, sum(s[1] * jnp.exp(s[0] - top) for s in shares), sum(s[2] for s in shares)
+    return top + jnp.log(sum(jnp.exp(s[0] - top) for s in shares)), sum(s[1] for s in shares)
 
 
 def kernel(
@@ -134,8 +134,14 @@
         if o == 1:
             send_weights(0, 1)
             w_copy(to_near, count, *spans[count]).start()
+
+            @pl.when((d == 0) | (d == NZ - 1))
+            def _():
+                for j in (2, from_near):
+                    w_copy(j, count, *spans[count]).start()
+
         if o == 2:
-            send_weights(1, AHEAD)
+            send_weights(1, count)
 
     for o in (0,) + OFFSETS:
         s = d + o
@@ -177,7 +183,6 @@
     blocks = NZ * per
     hw = 2 * width
     near = pl.ds(pl.multiple_of(d // 2 * hw, hw), hw)
-    far = pl.ds(pl.multiple_of((1 - d // 2) * hw, hw), hw)
 
     def load(src, c0, size, cols, k):
         return pltpu.make_async_copy(src.at[pl.ds(pl.multiple_of(c0, 16), size), cols], wb.at[pl.ds(0, size), cols], ld_sem.at[k])
@@ -190,6 +195,9 @@
 
     def column(j):
         return pl.ds(pl.multiple_of(lax.rem(d + NZ - j, NZ) * width, width), width)
+
+    from_inner = lax.rem(d + NZ - (2 - d // 2), NZ)
+    from_outer = lax.rem(d + NZ - (3 - 3 * (d // 2)), NZ)
 
     def block_of(n):
         return pl.ds(pl.multiple_of(n * BLOCK, BLOCK), BLOCK)
@@ -228,15 +236,17 @@
         fold(blocks - 1, c0, size, odd, last)
 
     t0 = count * big
-    loads = [load_own(t0, tail), load(land_ref, t0, tail, column(from_near), 1)]
-    w_copy(from_near, count, t0, tail).wait_recv()
+    loads = [load_own(t0, tail)]
+    for k, j in enumerate((from_near, from_outer)):
+        w_copy(j, count, t0, tail).wait_recv()
+        loads.append(load(land_ref, t0, tail, column(j), 1 + k))
     for copy in loads:
         copy.start()
     for copy in loads:
         copy.wait()
 
     def first_half(n, carry):
-        part_acc[:, block_of(n)] = product(n, tail, near)
+        part_acc[:, block_of(n)] = product(n, tail, near) + product(n, tail, column(from_outer))
         return carry
 
     lax.fori_loop(0, blocks, first_half, 0)
@@ -249,14 +259,8 @@
             w_copy(j, c, c0, big).wait_recv()
             loads.append(load(land_ref, c0, big, column(j), j))
             loads[-1].start()
-        ahead = c + AHEAD
-
-        @pl.when(ahead < count)
-        def _():
-            for j in (2, 1, 3):
-                w_copy(j, ahead, ahead * big, big).start()
-
-        @pl.when(ahead == count)
+
+        @pl.when((c + LATE == count) & (d > 0) & (d < NZ - 1))
         def _():
             for j in (2, from_near):
                 w_copy(j, count, t0, tail).start()
@@ -272,14 +276,13 @@
 
     lax.fori_loop(0, count, big_chunk, 0)
 
-    for j in (2, to_near):
-        w_copy(j, count, t0, tail).wait_recv()
-    rest = load(land_ref, t0, tail, far, 1)
+    w_copy(from_inner, count, t0, tail).wait_recv()
+    rest = load(land_ref, t0, tail, column(from_inner), 1)
     rest.start()
     rest.wait()
 
     def fill_rest(n, ref):
-        ref[pl.ds(0, tail), :] = part_acc[:, block_of(n)] + product(n, tail, far)
+        ref[pl.ds(0, tail), :] = part_acc[:, block_of(n)] + product(n, tail, column(from_inner))
 
     sweep(t0, tail, fill_rest, True)
 
@@ -291,7 +294,8 @@
         cols = pl.ds(t * slab, slab)
         tops = m_acc[:, cols]
         top = jnp.max(tops, axis=0, keepdims=True)
-        put(stats, t, top, jnp.sum(s_acc[:, cols] * jnp.exp(tops - top), axis=0, keepdims=True), jnp.sum(p_acc[:, cols], axis=0, keepdims=True))
+        total = jnp.sum(s_acc[:, cols] * jnp.exp(tops - top), axis=0, keepdims=True)
+        put(stats, t, top + jnp.log(total), jnp.sum(p_acc[:, cols], axis=0, keepdims=True))
 
     for idx, span in enumerate(spans):
         for j in (1, 2, 3):
@@ -338,8 +342,8 @@
         mx_copy(k).start()
     for k in range(1, NM):
         mx_copy(k).wait()
-    top, total, picked = merge([gat[k] for k in range(NM)])
-    log_prob = picked - top - jnp.log(total)
+    lse, picked = merge([gat[k] for k in range(NM)])
+    log_prob = picked - lse
     logp_ref[...] = log_prob
     accept_ref[...] = jnp.minimum(1.0, jnp.exp(log_prob) / q_ref[...])
 
@@ -378,9 +382,9 @@
                 pltpu.VMEM((big, BLOCK), jnp.float32),
                 pltpu.VMEM((big, BLOCK), jnp.float32),
                 pltpu.VMEM((piece - count * big, rows), jnp.float32),
-                pltpu.VMEM((NZ, 1, 3 * slab), jnp.float32),
-                pltpu.VMEM((NZ - 1, 1, 3 * slab), jnp.float32),
-                pltpu.VMEM((NM, 1, 3 * slab), jnp.float32),
+                pltpu.VMEM((NZ, 1, 2 * slab), jnp.float32),
+                pltpu.VMEM((NZ - 1, 1, 2 * slab), jnp.float32),
+                pltpu.VMEM((NM, 1, 2 * slab), jnp.float32),
                 dma((NZ - 1,)), dma((NZ - 1,)), dma((NM - 1,)), dma((NM - 1,)),
                 dma((2,)), dma((3,)), dma((3,)), dma((NZ + 1,)), dma((NZ,)),
                 dma((NZ,)), dma((NZ,)), dma((NZ,)), dma((NZ,)),

time: 630 us -> 628 us (level)
  no operation moved by 1% of the time
where the time goes in v3:
time: 628 us
  Pallas kernels  624 us (99%)
    pallas_call x1, Pallas kernels, per_device(): pl.pallas_call(functools.partial(kernel, cfg), out_shape=(jax.ShapeDtypeS...  624 us

profile of v3, /device:TPU:0, one launch (start us, length us, event | category | flops | bytes accessed | tf_op | source)
XLA Modules:
  0.0 627.6 jit_solution(13828140023634191154)
XLA Ops:
  0.6 624.4 %shard_map.59 = (f32[1,2048]{1,0:T(1,128)}, f32[1,2048]{1,0:T(1,128)}, bf16[4016,3072]{1,0:T(8,128)(2,1)}) custom-call(bf16[2048,384]{1,0:T(8,128)(2,1)} %h_ref.1, bf16[16032,768]{1,0:T(8,128)(2,1)} %w_ref.1, s32[1,2048]{1,0:T(1,128)} %bitcast.4, f32[1,2048]{1,0:T(1,128)} %bitcast.5), custom_call_target="tpu_custom_call" | custom-call | tf_op jit(solution)/shard_map/pallas_call | solution.py:362
  625.0 1.3 copy.8
  626.3 1.3 copy.9
